TPU v7x, 512 devices: a whole 4x4x16 slice. The times are simulated.
512 devices in a mesh: outer: 32 (over y, z_hi, core), inner: 16 (over z_lo, x).
Axes of the slice: x: 4, y: 4, z: 16 (z_hi: 4, z_lo: 4; z = z_hi * 4 + z_lo), core: 2. Of those that a mesh axis runs over, the one named last changes fastest.
Arguments:
- group_latents: bfloat16 [65536, 1024], P(('outer', 'inner')), may hold values from -6 to 6
- slot_ids: int32 [32, 16], P('outer', 'inner'), may hold values from 0 to 15, each once within a row
- slot_embed: bfloat16 [16, 1024], replicated, may hold values from -6 to 6
- merge_latents: bfloat16 [128, 2048], replicated, may hold values from -6 to 6
- query_weight: bfloat16 [2048, 2048], P(None, 'inner'), may hold values from -0.125 to 0.125
- key_weight: bfloat16 [1024, 2048], P(None, 'inner'), may hold values from -0.1875 to 0.1875
- value_weight: bfloat16 [1024, 2048], P(None, 'inner'), may hold values from -0.1875 to 0.1875
- output_weight: bfloat16 [2048, 2048], P('inner'), may hold values from -0.125 to 0.125
- global_latents: bfloat16 [1024, 2048], P(('outer', 'inner')), may hold values from -6 to 6
- decode_query: bfloat16 [2048, 2048], P(None, 'inner'), may hold values from -0.125 to 0.125
- decode_key: bfloat16 [2048, 2048], P(None, 'inner'), may hold values from -0.125 to 0.125
- decode_value: bfloat16 [2048, 2048], P(None, 'inner'), may hold values from -0.125 to 0.125
- decode_output: bfloat16 [2048, 2048], P('inner'), may hold values from -0.125 to 0.125
Outputs:
- decoded: bfloat16 [4096, 2048], P(('outer', 'inner'))
Inputs may be any that keep to these rules, and one draw needn't show every extreme that they name: `slot_ids`: each row holds every slot once.
All inputs are finite; a program needn't handle non-finite values.
Results may differ from a plain program's by a relative error of at most 0.014.
Values may be sent and summed in bfloat16 or wider, within the bound.
No kernel may reach another device: no remote copies, remote signals or barrier semaphores. Data moves between devices by JAX's collectives and lax.ppermute only.
A program may use at most 64 MiB of HBM per device.

v0:
```python
import jax
import jax.numpy as jnp
from jax import lax
from jax.sharding import Mesh
from jax.sharding import PartitionSpec as P

HEAD = 128
INNER = ("inner_0", "inner_1")
OUTER_INNER = ("outer", "inner_0", "inner_1")


def laid_out(tiles, dim):
    shape = list(tiles.shape[1:])
    shape[dim] *= tiles.shape[0]
    return jnp.moveaxis(tiles, 0, dim).reshape(shape)


def stacked_from(value, axes, order):
    tiles = value[None]
    for k in order:
        tiles = lax.all_gather(tiles, axes[k], axis=0, tiled=True)
    carried = [lax.axis_size(axes[k]) for k in reversed(order)]
    tiles = tiles.reshape(*carried, *value.shape)
    turned = sorted(range(len(order)), key=lambda place: order[len(order) - 1 - place])
    return tiles.transpose(*turned, *range(len(order), tiles.ndim)).reshape(-1, *value.shape)


def whole_of(value, axes, order, dim):
    return laid_out(stacked_from(value, axes, order), dim)


def filled_up(lines, size):
    spare = -len(lines) % size
    return jnp.pad(lines, [(0, spare)] + [(0, 0)] * (lines.ndim - 1))


def sum_in_two_steps(value, axis):
    lines = value.reshape(-1, *value.shape[1:][-1:])
    padded = filled_up(lines, lax.axis_size(axis))
    own = lax.psum_scatter(padded, axis, scatter_dimension=0, tiled=True)
    whole = lax.all_gather(own, axis, axis=0, tiled=True)
    return whole[: len(lines)].reshape(value.shape)


def copy_for_each(value, axis):
    copies = jnp.broadcast_to(value, (lax.axis_size(axis), *value.shape))
    return lax.all_to_all(copies, axis, split_axis=0, concat_axis=0, tiled=True)


def gather_directly(value, axis, dim):
    return laid_out(copy_for_each(value, axis), dim)


def in_blocks(value, dim, size):
    before, after = (value.shape[:dim], value.shape[dim + 1 :])
    return jnp.moveaxis(value.reshape(*before, size, -1, *after), dim, 0)


def sent_and_summed(value, axis, dim):
    tiles = in_blocks(value, dim, lax.axis_size(axis))
    arrived = lax.all_to_all(tiles, axis, split_axis=0, concat_axis=0, tiled=True)
    return arrived.astype(jnp.float32).sum(axis=0)


def attend(query_rows, key_rows, value_rows):
    length = query_rows.shape[0]
    head_count = query_rows.shape[1] // HEAD
    queries = query_rows.reshape(length, head_count, HEAD)
    keys_in = key_rows.reshape(key_rows.shape[0], head_count, HEAD)
    values_in = value_rows.reshape(value_rows.shape[0], head_count, HEAD)
    scores = jnp.einsum(
        "qhd,khd->hqk", queries, keys_in, preferred_element_type=jnp.float32
    ) * HEAD ** (-0.5)
    weights = jax.nn.softmax(scores, axis=-1).astype(jnp.bfloat16)
    mixed = jnp.einsum("hqk,khd->qhd", weights, values_in, preferred_element_type=jnp.float32)
    return mixed.reshape(length, head_count * HEAD).astype(jnp.bfloat16)


def local(
    group_latents,
    slot_ids,
    slot_embed,
    merge_latents,
    query_weight,
    key_weight,
    value_weight,
    output_weight,
    global_latents,
    decode_query,
    decode_key,
    decode_value,
    decode_output,
):
    columns = query_weight.shape[1]
    selector = (jnp.arange(slot_embed.shape[0], dtype=jnp.int32) == slot_ids[0, 0]).astype(
        jnp.bfloat16
    )
    slot_vector = jnp.dot(selector[None, :], slot_embed, preferred_element_type=jnp.float32)
    keyed = (group_latents.astype(jnp.float32) + slot_vector).astype(jnp.bfloat16)
    pair_two = jnp.concatenate([key_weight, value_weight], axis=1)
    keys_values = jnp.dot(
        whole_of(keyed, INNER, (0, 1), 0), pair_two, preferred_element_type=jnp.float32
    ).astype(jnp.bfloat16)
    query_two = jnp.dot(merge_latents, query_weight, preferred_element_type=jnp.float32).astype(
        jnp.bfloat16
    )
    mixed_two = attend(query_two, keys_values[:, :columns], keys_values[:, columns:])
    partial_value = jnp.dot(mixed_two, output_weight, preferred_element_type=jnp.float32)
    level_two = merge_latents.astype(jnp.float32) + sum_in_two_steps(
        partial_value.astype(jnp.bfloat16), INNER
    ).astype(jnp.float32)
    normed = (
        level_two * lax.rsqrt(jnp.mean(level_two * level_two, axis=-1, keepdims=True) + 1e-06)
    ).astype(jnp.bfloat16)
    query_five = jnp.dot(normed, decode_query, preferred_element_type=jnp.float32).astype(
        jnp.bfloat16
    )
    pair_five = jnp.concatenate([decode_key, decode_value], axis=1)
    outer_block = gather_directly(global_latents, INNER, 0)
    global_pairs = gather_directly(
        jnp.dot(outer_block, pair_five, preferred_element_type=jnp.float32).astype(jnp.bfloat16),
        "outer",
        0,
    )
    mixed_five = attend(query_five, global_pairs[:, :columns], global_pairs[:, columns:])
    own_rows = merge_latents.shape[0] // lax.axis_size(INNER)
    summed = sent_and_summed(
        jnp.dot(mixed_five, decode_output, preferred_element_type=jnp.float32).astype(jnp.bfloat16),
        INNER,
        0,
    )
    own_part = lax.dynamic_slice_in_dim(level_two, lax.axis_index(INNER) * own_rows, own_rows, 0)
    return (own_part + summed).astype(jnp.bfloat16)


def solution(mesh):
    finer = Mesh(mesh.devices.reshape(mesh.shape["outer"], 4, 4), ("outer", "inner_0", "inner_1"))
    placed = (
        P(OUTER_INNER, None),
        P("outer", INNER),
        P(),
        P(),
        P(None, INNER),
        P(None, INNER),
        P(None, INNER),
        P(INNER, None),
        P(OUTER_INNER, None),
        P(None, INNER),
        P(None, INNER),
        P(None, INNER),
        P(INNER, None),
    )
    return jax.shard_map(
        local, mesh=finer, in_specs=placed, out_specs=P(OUTER_INNER, None), check_vma=False
    )
```

profile of v0, /device:TPU:2, one launch (start us, length us, event | category | flops | bytes accessed | tf_op | source)
XLA Modules:
  0.0 278.3 jit_solution(5552912724020188070)
XLA Ops:
  7.2 0.9 fusion.28
  8.1 1.7 add_convert_fusion
  9.8 0.0 all-gather.6.cloned.1.call-update
  9.8 0.0 all-gather.4.cloned.1.call-start
  9.9 43.3 %all-gather.6.cloned.1.call-done = bf16[512,1024]{1,0:T(8,128)(2,1)} async-done(((bf16[128,1024]{1,0:T(8,128)(2,1)}), bf16[512,1024]{1,0:T(8,128)(2,1)}) %all-gather.6.cloned.1.call-update) | async-done | bytes 1048592 | tf_op jit(solution)/shard_map/all_gather | solution.py:21
  53.2 0.0 all-gather.4.cloned.1.call-update
  53.2 0.8 broadcast_in_dim.7
  53.9 12.5 %all_to_all.15 = bf16[16,2,2048]{2,1,0:T(2,128)(2,1)S(1)} all-to-all(bf16[16,2,2048]{2,1,0:T(2,128)(2,1)S(1)} %broadcast_in_dim.7), channel_id=1, replica_groups=mesh['outer'=32,'inner_0'=4,'inner_1'=4] {'inner_0','inner_1'}, dimensions={0} | all-to-all | bytes 262144 | tf_op jit(solution)/shard_map/all_to_all | solution.py:47
  66.5 0.1 reshape.87
  66.5 1.5 fusion.3
  68.0 0.9 broadcast_in_dim.8
  68.9 14.9 %all-to-all-start.1 = ((bf16[32,32,256]{2,1,0:T(8,128)(2,1)}), bf16[32,32,256]{2,1,0:T(8,128)(2,1)}, u32[]{:S(2)}, u32[]{:S(2)}) async-start(bf16[32,32,256]{2,1,0:T(8,128)(2,1)} %broadcast_in_dim.8), calls=%async_computation.2 | async-start | bytes 1048576 | tf_op jit(solution)/shard_map/all_to_all | solution.py:47
  83.8 0.0 reduce-scatter.2.cloned.1.call-start
  83.8 25.6 %all-gather.4.cloned.1.call-done = bf16[16,128,1024]{2,1,0:T(8,128)(2,1)} async-done(((bf16[4,128,1024]{2,1,0:T(8,128)(2,1)}), bf16[16,128,1024]{2,1,0:T(8,128)(2,1)}) %all-gather.4.cloned.1.call-update) | async-done | bytes 4194320 | tf_op jit(solution)/shard_map/all_gather | solution.py:21
  109.5 2.7 copy.15
  112.2 0.0 copy-start.1
  112.2 1.3 convolution_convert_fusion
  113.5 0.6 fusion.35
  114.1 0.3 fusion.7
  114.4 2.8 convolution_convert_fusion.2
  117.2 0.0 reduce-scatter.2.cloned.1.call-update
  117.2 87.4 %reduce-scatter.2.cloned.1.call-done = bf16[8,2048]{1,0:T(8,128)(2,1)} async-done(((bf16[128,2048]{1,0:T(8,128)(2,1)}), bf16[8,2048]{1,0:T(8,128)(2,1)}) %reduce-scatter.2.cloned.1.call-update) | async-done | bytes 32784 | tf_op jit(solution)/shard_map/reduce_scatter | solution.py:40
  204.6 44.8 %all_gather.11 = bf16[128,2048]{1,0:T(8,128)(2,1)S(1)} all-gather(bf16[8,2048]{1,0:T(8,128)(2,1)} %reduce-scatter.2.cloned.1.call-done), channel_id=1, replica_groups=mesh['outer'=32,'inner_0'=4,'inner_1'=4] {'inner_0','inner_1'}, dimensions={0}, use_global_device_ids=true | all-gather | bytes 557056 | tf_op jit(solution)/shard_map/all_gather | solution.py:41
  249.3 0.3 convert_add_fusion
  249.6 0.0 all-to-all-done.1
  249.6 1.7 fusion.36
  251.4 0.2 fusion.20
  251.6 2.7 fusion
  254.3 5.8 %all-to-all-start.2 = ((bf16[16,8,2048]{2,1,0:T(8,128)(2,1)}), bf16[16,8,2048]{2,1,0:T(8,128)(2,1)S(1)}, u32[]{:S(2)}, u32[]{:S(2)}) async-start(bf16[16,8,2048]{2,1,0:T(8,128)(2,1)} %fusion), calls=%async_computation.3 | async-start | bytes 1048576 | tf_op jit(solution)/shard_map/all_to_all | solution.py:61
  260.1 11.0 %all-to-all-done.2 = bf16[16,8,2048]{2,1,0:T(8,128)(2,1)S(1)} async-done(((bf16[16,8,2048]{2,1,0:T(8,128)(2,1)}), bf16[16,8,2048]{2,1,0:T(8,128)(2,1)S(1)}, u32[]{:S(2)}, u32[]{:S(2)}) %all-to-all-start.2) | async-done | bytes 524320 | tf_op jit(solution)/shard_map/all_to_all | solution.py:61
  271.1 0.1 convert_reduce_fusion
  271.2 0.6 add_convert_fusion.1
  (9 shorter events, 0.0 us)
Async XLA Ops:
  6.5 106.9 %copy-start = (bf16[2048,128]{1,0:T(8,128)(2,1)S(1)}, bf16[2048,128]{1,0:T(8,128)(2,1)}, u32[]{:S(2)}) copy-start(bf16[2048,128]{1,0:T(8,128)(2,1)} %param.17) | copy-start | bytes 1572868
  6.5 46.6 %all-gather.6.cloned.1.call-start = ((), (), s32[]{:S(2)}) async-start(), calls=%async_computation.6 | async-start | bytes 1310720 | tf_op jit(solution)/shard_map/all_gather | solution.py:21
  9.8 99.6 %all-gather.4.cloned.1.call-start = ((), (), s32[]{:S(2)}) async-start(), calls=%async_computation.4 | async-start | bytes 5242880 | tf_op jit(solution)/shard_map/all_gather | solution.py:21
  68.9 180.7 %all-to-all-start.1 = ((bf16[32,32,256]{2,1,0:T(8,128)(2,1)}), bf16[32,32,256]{2,1,0:T(8,128)(2,1)}, u32[]{:S(2)}, u32[]{:S(2)}) async-start(bf16[32,32,256]{2,1,0:T(8,128)(2,1)} %broadcast_in_dim.8), calls=%async_computation.2 | async-start | bytes 1048576 | tf_op jit(solution)/shard_map/all_to_all | solution.py:47
  83.8 120.8 %reduce-scatter.2.cloned.1.call-start = ((), (), s32[]{:S(2)}) async-start(), calls=%async_computation.5 | async-start | bytes 557056 | tf_op jit(solution)/shard_map/reduce_scatter | solution.py:40
  109.5 2.7 copy-start.2
  109.5 2.7 copy-start.3
  112.2 1.3 copy-start.1
  254.3 16.8 %all-to-all-start.2 = ((bf16[16,8,2048]{2,1,0:T(8,128)(2,1)}), bf16[16,8,2048]{2,1,0:T(8,128)(2,1)S(1)}, u32[]{:S(2)}, u32[]{:S(2)}) async-start(bf16[16,8,2048]{2,1,0:T(8,128)(2,1)} %fusion), calls=%async_computation.3 | async-start | bytes 1048576 | tf_op jit(solution)/shard_map/all_to_all | solution.py:61
Sparse Core Ops, SparseCore 0:
  10.0 43.1 all-gather.5
  55.2 54.1 all-gather.3
  117.3 87.2 reduce-scatter.1
where the time goes:
time: 279 us; the launch traced here: 278 us
  waiting for transfers between devices  167 us (60%)
  blocking collectives  57.3 us (21%)
  starting transfers between devices  20.8 us (7%)
  between operations  13.9 us (5%)
  matrix products  11.4 us (4%)
  local copies, waits for them, and re-layouts  4.41 us (2%)
  other arithmetic  3.21 us (1%)
    reduce_scatter x1, waiting for transfers between devices, sum_in_two_steps(): own = lax.psum_scatter(padded, axis, scatter_dimension=0, tiled=True)  87.4 us
    all_gather x2, waiting for transfers between devices, stacked_from(): tiles = lax.all_gather(tiles, axes[k], axis=0, tiled=True)  68.9 us
    all_gather x1, blocking collectives, sum_in_two_steps(): whole = lax.all_gather(own, axis, axis=0, tiled=True)  44.8 us
    all_to_all x1, starting transfers between devices, copy_for_each(): return lax.all_to_all(copies, axis, split_axis=0, concat_axis=0, tiled=True)  14.9 us
    all_to_all x1, blocking collectives, copy_for_each(): return lax.all_to_all(copies, axis, split_axis=0, concat_axis=0, tiled=True)  12.5 us
    all_to_all x1, waiting for transfers between devices, sent_and_summed(): lax.all_to_all(tiles, axis, split_axis=0, concat_axis=0, tiled=True)  11 us
    all_to_all x1, starting transfers between devices, sent_and_summed(): lax.all_to_all(tiles, axis, split_axis=0, concat_axis=0, tiled=True)  5.83 us
  transfers between devices with their start and end apart: 5, of which 4 were waited for; matrix products, arithmetic and copies ran while one was open for 4% of the time, Pallas kernels for 0%

commit v1 on v0

--- a/solution.py
+++ b/solution.py
@@ -7,6 +7,13 @@
 HEAD = 128
 INNER = ("inner_0", "inner_1")
 OUTER_INNER = ("outer", "inner_0", "inner_1")
+
+
+def gather_over(x, name, d):
+    size = lax.axis_size(name)
+    blocks = jnp.stack([x for _ in range(size)])
+    blocks = lax.all_to_all(blocks, name, split_axis=0, concat_axis=0)
+    return jnp.concatenate(blocks, axis=d)
 
 
 def laid_out(tiles, dim):
@@ -38,7 +45,7 @@
     lines = value.reshape(-1, *value.shape[1:][-1:])
     padded = filled_up(lines, lax.axis_size(axis))
     own = lax.psum_scatter(padded, axis, scatter_dimension=0, tiled=True)
-    whole = lax.all_gather(own, axis, axis=0, tiled=True)
+    whole = gather_over(own, axis, 0)
     return whole[: len(lines)].reshape(value.shape)
 
 

time: 279 us -> 306 us (1.097)
  the two profiles are of different devices: /device:TPU:2 before, /device:TPU:32 now
where the time goes in v1:
time: 306 us; the launch traced here: 305 us
  waiting for transfers between devices  227 us (74%)
  starting transfers between devices  30.3 us (10%)
  between operations  13.9 us (5%)
  blocking collectives  13.5 us (4%)
  matrix products  11.4 us (4%)
  local copies, waits for them, and re-layouts  6.07 us (2%)
  other arithmetic  3.21 us (1%)
    all_gather x2, waiting for transfers between devices, stacked_from(): tiles = lax.all_gather(tiles, axes[k], axis=0, tiled=True)  99.8 us
    reduce_scatter x1, waiting for transfers between devices, sum_in_two_steps(): own = lax.psum_scatter(padded, axis, scatter_dimension=0, tiled=True)  70.1 us
    all_to_all x1, waiting for transfers between devices, copy_for_each(): return lax.all_to_all(copies, axis, split_axis=0, concat_axis=0, tiled=True)  33.6 us
    all_to_all x1, waiting for transfers between devices, sent_and_summed(): lax.all_to_all(tiles, axis, split_axis=0, concat_axis=0, tiled=True)  14.6 us
    all_to_all x1, blocking collectives, copy_for_each(): return lax.all_to_all(copies, axis, split_axis=0, concat_axis=0, tiled=True)  13.5 us
    all_to_all x1, starting transfers between devices, copy_for_each(): return lax.all_to_all(copies, axis, split_axis=0, concat_axis=0, tiled=True)  13.2 us
    all_to_all x1, starting transfers between devices, gather_over(): blocks = lax.all_to_all(blocks, name, split_axis=0, concat_axis=0)  11.3 us
    all_to_all x1, waiting for transfers between devices, gather_over(): blocks = lax.all_to_all(blocks, name, split_axis=0, concat_axis=0)  8.75 us
  transfers between devices with their start and end apart: 6, of which 6 were waited for; matrix products, arithmetic and copies ran while one was open for 1% of the time, Pallas kernels for 0%

profile of v1, /device:TPU:32, one launch (start us, length us, event | category | flops | bytes accessed | tf_op | source)
XLA Modules:
  0.0 305.3 jit_solution(3006097944056025172)
XLA Ops:
  7.2 0.9 fusion.28
  8.1 1.7 add_convert_fusion
  9.8 0.0 all-gather.6.cloned.1.call-update
  9.8 0.0 all-gather.4.cloned.1.call-start
  9.9 40.9 %all-gather.6.cloned.1.call-done = bf16[512,1024]{1,0:T(8,128)(2,1)} async-done(((bf16[128,1024]{1,0:T(8,128)(2,1)}), bf16[512,1024]{1,0:T(8,128)(2,1)}) %all-gather.6.cloned.1.call-update) | async-done | bytes 1048592 | tf_op jit(solution)/shard_map/all_gather | solution.py:28
  50.8 0.0 reduce-scatter.2.cloned.1.call-start
  50.9 58.9 %all-gather.4.cloned.1.call-done = bf16[16,128,1024]{2,1,0:T(8,128)(2,1)} async-done(((bf16[4,128,1024]{2,1,0:T(8,128)(2,1)}), bf16[16,128,1024]{2,1,0:T(8,128)(2,1)}) %all-gather.4.cloned.1.call-update) | async-done | bytes 4194320 | tf_op jit(solution)/shard_map/all_gather | solution.py:28
  109.7 2.7 copy.15
  112.5 1.3 convolution_convert_fusion
  113.8 0.6 fusion.35
  114.4 0.3 fusion.7
  114.7 2.8 convolution_convert_fusion.2
  117.5 0.1 broadcast_in_dim.7
  117.6 13.5 %all_to_all.20 = bf16[16,2,2048]{2,1,0:T(2,128)(2,1)S(1)} all-to-all(bf16[16,2,2048]{2,1,0:T(2,128)(2,1)S(1)} %broadcast_in_dim.7), channel_id=1, replica_groups=mesh['outer'=32,'inner_0'=4,'inner_1'=4] {'inner_0','inner_1'}, dimensions={0} | all-to-all | bytes 262144 | tf_op jit(solution)/shard_map/all_to_all | solution.py:54
  131.1 70.1 %reduce-scatter.2.cloned.1.call-done = bf16[8,2048]{1,0:T(8,128)(2,1)} async-done(((bf16[128,2048]{1,0:T(8,128)(2,1)}), bf16[8,2048]{1,0:T(8,128)(2,1)}) %reduce-scatter.2.cloned.1.call-update) | async-done | bytes 32784 | tf_op jit(solution)/shard_map/reduce_scatter | solution.py:47
  201.2 1.6 stack.2
  202.8 11.3 %all-to-all-start = ((bf16[16,8,2048]{2,1,0:T(8,128)(2,1)}), bf16[16,8,2048]{2,1,0:T(8,128)(2,1)S(1)}, u32[]{:S(2)}, u32[]{:S(2)}) async-start(bf16[16,8,2048]{2,1,0:T(8,128)(2,1)} %stack.2), calls=%async_computation.1 | async-start | bytes 1048576 | tf_op jit(solution)/shard_map/all_to_all | solution.py:15
  214.1 0.1 reshape.92
  214.2 1.5 fusion.3
  215.7 8.8 %all-to-all-done = bf16[16,8,2048]{2,1,0:T(8,128)(2,1)S(1)} async-done(((bf16[16,8,2048]{2,1,0:T(8,128)(2,1)}), bf16[16,8,2048]{2,1,0:T(8,128)(2,1)S(1)}, u32[]{:S(2)}, u32[]{:S(2)}) %all-to-all-start) | async-done | bytes 524320 | tf_op jit(solution)/shard_map/all_to_all | solution.py:15
  224.4 0.8 broadcast_in_dim.8
  225.3 13.2 %all-to-all-start.2 = ((bf16[32,32,256]{2,1,0:T(8,128)(2,1)}), bf16[32,32,256]{2,1,0:T(8,128)(2,1)S(1)}, u32[]{:S(2)}, u32[]{:S(2)}) async-start(bf16[32,32,256]{2,1,0:T(8,128)(2,1)} %broadcast_in_dim.8), calls=%async_computation.3 | async-start | bytes 1048576 | tf_op jit(solution)/shard_map/all_to_all | solution.py:54
  238.5 0.3 convert_add_fusion
  238.8 33.6 %all-to-all-done.2 = bf16[32,32,256]{2,1,0:T(8,128)(2,1)S(1)} async-done(((bf16[32,32,256]{2,1,0:T(8,128)(2,1)}), bf16[32,32,256]{2,1,0:T(8,128)(2,1)S(1)}, u32[]{:S(2)}, u32[]{:S(2)}) %all-to-all-start.2) | async-done | bytes 524320 | tf_op jit(solution)/shard_map/all_to_all | solution.py:54
  272.4 0.8 copy-done.2
  273.2 1.7 fusion.36
  274.9 0.2 fusion.20
  275.1 2.7 fusion
  277.8 5.7 %all-to-all-start.3 = ((bf16[16,8,2048]{2,1,0:T(8,128)(2,1)}), bf16[16,8,2048]{2,1,0:T(8,128)(2,1)S(1)}, u32[]{:S(2)}, u32[]{:S(2)}) async-start(bf16[16,8,2048]{2,1,0:T(8,128)(2,1)} %fusion), calls=%async_computation.4 | async-start | bytes 1048576 | tf_op jit(solution)/shard_map/all_to_all | solution.py:68
  283.4 14.6 %all-to-all-done.3 = bf16[16,8,2048]{2,1,0:T(8,128)(2,1)S(1)} async-done(((bf16[16,8,2048]{2,1,0:T(8,128)(2,1)}), bf16[16,8,2048]{2,1,0:T(8,128)(2,1)S(1)}, u32[]{:S(2)}, u32[]{:S(2)}) %all-to-all-start.3) | async-done | bytes 524320 | tf_op jit(solution)/shard_map/all_to_all | solution.py:68
  298.0 0.1 convert_reduce_fusion
  298.1 0.6 add_convert_fusion.1
  (15 shorter events, 0.1 us)
Async XLA Ops:
  6.5 107.2 %copy-start = (bf16[2048,128]{1,0:T(8,128)(2,1)S(1)}, bf16[2048,128]{1,0:T(8,128)(2,1)}, u32[]{:S(2)}) copy-start(bf16[2048,128]{1,0:T(8,128)(2,1)} %param.17) | copy-start | bytes 1572868
  6.5 44.3 %all-gather.6.cloned.1.call-start = ((), (), s32[]{:S(2)}) async-start(), calls=%async_computation.7 | async-start | bytes 1310720 | tf_op jit(solution)/shard_map/all_gather | solution.py:28
  9.8 99.9 %all-gather.4.cloned.1.call-start = ((), (), s32[]{:S(2)}) async-start(), calls=%async_computation.5 | async-start | bytes 5242880 | tf_op jit(solution)/shard_map/all_gather | solution.py:28
  50.8 150.4 %reduce-scatter.2.cloned.1.call-start = ((), (), s32[]{:S(2)}) async-start(), calls=%async_computation.6 | async-start | bytes 557056 | tf_op jit(solution)/shard_map/reduce_scatter | solution.py:47
  109.7 2.7 copy-start.4
  109.7 2.7 copy-start.5
  112.4 1.3 copy-start.1
  113.8 3.7 %copy-start.3 = (bf16[2,2048]{1,0:T(2,128)(2,1)S(1)}, bf16[2,2048]{1,0:T(2,128)(2,1)}, u32[]{:S(2)}) copy-start(bf16[2,2048]{1,0:T(2,128)(2,1)} %param.21) | copy-start | bytes 24580
  202.8 21.6 %all-to-all-start = ((bf16[16,8,2048]{2,1,0:T(8,128)(2,1)}), bf16[16,8,2048]{2,1,0:T(8,128)(2,1)S(1)}, u32[]{:S(2)}, u32[]{:S(2)}) async-start(bf16[16,8,2048]{2,1,0:T(8,128)(2,1)} %stack.2), calls=%async_computation.1 | async-start | bytes 1048576 | tf_op jit(solution)/shard_map/all_to_all | solution.py:15
  225.3 47.1 %all-to-all-start.2 = ((bf16[32,32,256]{2,1,0:T(8,128)(2,1)}), bf16[32,32,256]{2,1,0:T(8,128)(2,1)S(1)}, u32[]{:S(2)}, u32[]{:S(2)}) async-start(bf16[32,32,256]{2,1,0:T(8,128)(2,1)} %broadcast_in_dim.8), calls=%async_computation.3 | async-start | bytes 1048576 | tf_op jit(solution)/shard_map/all_to_all | solution.py:54
  272.4 0.8 copy-start.2
  277.8 20.2 %all-to-all-start.3 = ((bf16[16,8,2048]{2,1,0:T(8,128)(2,1)}), bf16[16,8,2048]{2,1,0:T(8,128)(2,1)S(1)}, u32[]{:S(2)}, u32[]{:S(2)}) async-start(bf16[16,8,2048]{2,1,0:T(8,128)(2,1)} %fusion), calls=%async_computation.4 | async-start | bytes 1048576 | tf_op jit(solution)/shard_map/all_to_all | solution.py:68
Sparse Core Ops, SparseCore 0:
  10.0 40.7 all-gather.5
  52.9 56.7 all-gather.3
  117.6 83.5 reduce-scatter.1
